TPU v7x, 256 devices: a whole 4x4x8 slice. The times are simulated.
256 devices in a mesh: front: 32 (over z, x), panel: 8 (over y, core).
Axes of the slice: x: 4, y: 4, z: 8, core: 2. Of those that a mesh axis runs over, the one named last changes fastest.
Arguments:
- coupling: bfloat16 [32, 2048, 2048], P('front', 'panel'), may hold values from -1 to 1
- pivot_inverse: bfloat16 [32, 2048, 2048], P('front', 'panel'), may hold values from -0.125 to 0.125
- pivots: float32 [32, 2048], P('front'), as said below
- trailing: float32 [32, 2048, 2048], P('front', 'panel'), may hold values from -12 to 12
- sketch: float32 [32, 8, 8, 32, 256], P('front', 'panel'), may hold values from -6 to 6
- extend_map: int32 [32, 2048], replicated, may hold values from 0 to 511, as said below
- parent_of: int32 [32], replicated, may hold values from 0 to 31, as said below
- parent_base: bfloat16 [32, 4096, 4096], P('front', 'panel'), may hold values from -6 to 6
Outputs:
- assembled: bfloat16 [32, 4096, 4096], P('front', 'panel')
Inputs may be any that keep to these rules, and one draw needn't show every extreme that they name: `extend_map`: within each front and each aligned block of 2048 / 8 entries the values are distinct and rising. `pivots`: every entry's magnitude lies between 0.5 and 2 times 2048 ** -0.5; signs are mixed. `parent_of`: no parent has more than 4 children; some parent has exactly 4.
All inputs are finite; a program needn't handle non-finite values.
Results may differ from a plain program's by a relative error of at most 0.0043.
Values may be sent and summed in bfloat16 or wider, within the bound.
A program may use at most 128 MiB of HBM per device.

v0:
```python
import jax
import jax.numpy as jnp
from jax import lax
from jax.sharding import PartitionSpec as P

MAXKIDS = 4


def compress_rows(schur, omega, tile_rows, tile_cols, tile_size):
    tiles = schur.reshape(tile_rows, tile_size, tile_cols, tile_size)
    range_t = jnp.einsum("ijkb,iajb->ijka", omega, tiles, precision=lax.Precision.HIGHEST)
    gram = jnp.einsum("ijka,ijla->ijkl", range_t, range_t, precision=lax.Precision.HIGHEST)
    lower = jnp.linalg.cholesky(gram)
    basis = jax.scipy.linalg.solve_triangular(lower, range_t, lower=True)
    coeff = jnp.einsum("ijka,iajb->ijkb", basis, tiles, precision=lax.Precision.HIGHEST)
    return (basis.astype(jnp.bfloat16), coeff.astype(jnp.bfloat16))


def body(coupling, pivot_inverse, pivots, trailing, sketch, extend_map, parent_of, parent_base):
    rows_here = coupling[0]
    row_dev = rows_here.shape[0]
    factor_sum = jnp.dot(
        rows_here,
        lax.all_gather(pivot_inverse, "panel", axis=1, tiled=True)[0],
        preferred_element_type=jnp.float32,
    )
    factor = factor_sum.astype(jnp.bfloat16)
    scaled = (factor.astype(jnp.float32) / pivots[0][None, :]).astype(jnp.bfloat16)
    gathered = lax.all_gather(factor, "panel", axis=0, tiled=True)
    update = lax.dot_general(
        scaled, gathered, (((1,), (1,)), ((), ())), preferred_element_type=jnp.float32
    )
    schur = trailing[0] - update
    omega = sketch[0]
    tile_rows = omega.shape[0]
    tile_cols = omega.shape[1]
    tile_size = omega.shape[3]
    basis, coeff = compress_rows(schur, omega, tile_rows, tile_cols, tile_size)
    contrib = tile_cols * tile_size
    parent_dev = parent_base.shape[1]
    parent_width = parent_base.shape[2]
    panels = lax.axis_size("panel")
    owner = lax.axis_index("front")
    panel_here = lax.axis_index("panel")
    targets = jnp.arange(parent_dev, dtype=jnp.int32)
    sources = jnp.arange(row_dev, dtype=jnp.int32)
    offsets = jnp.arange(panels, dtype=jnp.int32) * row_dev
    empty = jnp.zeros((parent_dev, parent_width), jnp.float32)

    def place(total, child, basis_f, coeff_f):
        maps = extend_map[child]
        row_map = lax.dynamic_slice_in_dim(maps, panel_here * row_dev, row_dev, 0)
        match_rows = row_map[None, :] == targets[:, None]
        source_rows = jnp.sum(jnp.where(match_rows, sources[None, :], 0), axis=1)
        valid_rows = jnp.any(match_rows, axis=1)
        blocks = maps.reshape(panels, row_dev)
        match_cols = blocks[:, None, :] == targets[None, :, None]
        source_cols = (
            jnp.sum(jnp.where(match_cols, sources[None, None, :], 0), axis=2) + offsets[:, None]
        ).reshape(parent_width)
        valid_cols = jnp.any(match_cols, axis=2).reshape(parent_width)
        dense = jnp.einsum(
            "ijka,ijkb->iajb", basis_f, coeff_f, preferred_element_type=jnp.float32
        ).reshape(row_dev, contrib)
        picked = jnp.take(jnp.take(dense, source_rows, axis=0), source_cols, axis=1)
        return total + jnp.where(valid_rows[:, None] & valid_cols[None, :], picked, 0.0)

    fronts = parent_of.shape[0]
    front_ids = jnp.arange(fronts, dtype=jnp.int32)
    same_parent = parent_of[:, None] == parent_of[None, :]
    position = jnp.sum(
        jnp.where(same_parent & (front_ids[None, :] < front_ids[:, None]), 1, 0), axis=1
    ).astype(jnp.int32)
    slot_ids = jnp.arange(MAXKIDS, dtype=jnp.int32)
    matches = (parent_of[None, :, None] == front_ids[:, None, None]) & (
        position[None, :, None] == slot_ids[None, None, :]
    )
    children = jnp.sum(jnp.where(matches, front_ids[None, :, None], 0), axis=1)
    present = jnp.any(matches, axis=1)
    packed = jnp.stack((basis, coeff)).reshape(fronts, -1)
    spread = lax.all_to_all(packed, "front", split_axis=0, concat_axis=0, tiled=True)
    chosen = jnp.take(spread, children.reshape(-1), axis=0)
    outgoing = jnp.where(present.reshape(-1)[:, None], chosen, jnp.zeros((), jnp.bfloat16)).reshape(
        fronts, MAXKIDS, -1
    )
    received = lax.all_to_all(outgoing, "front", split_axis=0, concat_axis=2, tiled=True)
    kids_data = received[0].reshape((MAXKIDS, 2) + basis.shape)
    mine = present[owner]
    kid_ids = children[owner]

    def one_slot(item, acc):
        return lax.cond(
            mine[item],
            lambda inner: place(inner, kid_ids[item], kids_data[item, 0], kids_data[item, 1]),
            lambda inner: inner,
            acc,
        )

    gathered_sum = lax.fori_loop(0, MAXKIDS, one_slot, empty)
    assembled = (parent_base[0].astype(jnp.float32) + gathered_sum).astype(jnp.bfloat16)
    return assembled[None]


def solution(mesh):
    placed = (
        P("front", "panel", None),
        P("front", "panel", None),
        P("front", None),
        P("front", "panel", None),
        P("front", "panel", None, None, None),
        P(),
        P(),
        P("front", "panel", None),
    )
    return jax.shard_map(
        body, mesh=mesh, in_specs=placed, out_specs=P("front", "panel", None), check_vma=False
    )
```

profile of v0, /device:TPU:66, one launch (start us, length us, event | category | flops | bytes accessed | tf_op | source)
XLA Modules:
  0.0 490.0 jit_solution(11895995338993416951)
XLA Ops:
  7.3 56.4 %all-gather.3.cloned.1.call-done = bf16[1,2048,2048]{2,1,0:T(8,128)(2,1)} async-done(((bf16[1,256,2048]{2,1,0:T(8,128)(2,1)}), bf16[1,2048,2048]{2,1,0:T(8,128)(2,1)}) %all-gather.3.cloned.1.call-update) | async-done | bytes 8388624 | tf_op jit(solution)/shard_map/all_gather | solution.py:24
  63.7 6.7 %fusion.20 = bf16[256,2048]{1,0:T(8,128)(2,1)} fusion(bf16[1,2048,2048]{2,1,0:T(8,128)(2,1)} %all-gather.3.cloned.1.call-done, bf16[1,256,2048]{2,1,0:T(8,128)(2,1)S(1)} %copy-done), kind=kOutput, calls=%fused_computation.40 | convolution fusion | flops 2148007936 | bytes 10485760 | tf_op jit(solution)/shard_map/dot_general | solution.py:22
  70.8 52.2 %all-gather.5.cloned.1.call-done = bf16[2048,2048]{1,0:T(8,128)(2,1)} async-done(((bf16[256,2048]{1,0:T(8,128)(2,1)}), bf16[2048,2048]{1,0:T(8,128)(2,1)}) %all-gather.5.cloned.1.call-update) | async-done | bytes 8388624 | tf_op jit(solution)/shard_map/all_gather | solution.py:29
  123.0 6.7 %convolution_subtract_fusion = f32[256,2048]{1,0:T(8,128)S(1)} fusion(bf16[2048,2048]{1,0:T(8,128)(2,1)} %all-gather.5.cloned.1.call-done, f32[1,256,2048]{2,1,0:T(8,128)} %param.15, bf16[256,2048]{1,0:T(8,128)(2,1)} %fusion.20, f32[2048]{0:T(1024)S(1)} %bitcast.118), kind=kOutput, calls=%fused_computation.39 | convolution fusion | flops 2149580800 | bytes 13639680 | tf_op jit(solution)/shard_map/dot_general | solution.py:30
  129.7 2.0 fusion.25
  132.2 23.4 %custom-call.8 = f32[1,8,32,32]{3,2,1,0:T(8,128)S(1)} custom-call(f32[1,8,32,32]{3,2,1,0:T(8,128)S(1)} %fusion.38), custom_call_target="Cholesky" | custom-call | tf_op jit(solution)/shard_map/jit(cholesky)/cholesky | solution.py:13
  155.9 19.7 %custom-call.9 = f32[8,1,32,32]{2,3,1,0:T(8,128)S(1)} custom-call(f32[8,1,32,32]{3,2,1,0:T(8,128)S(1)} %select_bitcast_fusion), custom_call_target="InvertDiagBlocksLowerTriangular" | custom-call | tf_op jit(solution)/shard_map/jit(_solve_triangular)/vmap()/triangular_solve | solution.py:14
  178.1 2.2 reduce.17
  181.1 10.0 %all-to-all-start = ((bf16[32,2,2048]{2,1,0:T(2,128)(2,1)}), bf16[32,2,2048]{2,1,0:T(2,128)(2,1)S(1)}, u32[]{:S(2)}, u32[]{:S(2)}) async-start(bf16[32,2,2048]{2,1,0:T(2,128)(2,1)} %reshape.271), calls=%async_computation | async-start | bytes 524288 | tf_op jit(solution)/shard_map/all_to_all | solution.py:81
  191.7 10.2 %all-to-all-done = bf16[32,2,2048]{2,1,0:T(2,128)(2,1)S(1)} async-done(((bf16[32,2,2048]{2,1,0:T(2,128)(2,1)}), bf16[32,2,2048]{2,1,0:T(2,128)(2,1)S(1)}, u32[]{:S(2)}, u32[]{:S(2)}) %all-to-all-start) | async-done | bytes 262176 | tf_op jit(solution)/shard_map/all_to_all | solution.py:81
  205.8 6.5 %all-to-all-start.1 = ((bf16[32,4,4096]{2,1,0:T(4,128)(2,1)}), bf16[32,4,4096]{2,1,0:T(4,128)(2,1)S(1)}, u32[]{:S(2)}, u32[]{:S(2)}) async-start(bf16[32,4,4096]{2,1,0:T(4,128)(2,1)} %select_select_fusion), calls=%async_computation.1 | async-start | bytes 2097152 | tf_op jit(solution)/shard_map/all_to_all | solution.py:86
  212.7 24.9 %all-to-all-done.1 = bf16[32,4,4096]{2,1,0:T(4,128)(2,1)S(1)} async-done(((bf16[32,4,4096]{2,1,0:T(4,128)(2,1)}), bf16[32,4,4096]{2,1,0:T(4,128)(2,1)S(1)}, u32[]{:S(2)}, u32[]{:S(2)}) %all-to-all-start.1) | async-done | bytes 1048608 | tf_op jit(solution)/shard_map/all_to_all | solution.py:86
  238.7 4.3 broadcast_in_dim.118
  243.0 223.2 %while.18 = (s32[]{:T(128)}, f32[512,4096]{0,1:T(8,128)}, pred[4]{0:T(512)(128)(4,1)S(1)}, s32[4]{0:T(128)S(1)}, s32[]{:T(128)}, /*index=5*/s32[32,2048]{1,0:T(8...) while((s32[]{:T(128)}, f32[512,4096]{0,1:T(8,128)}, pred[4]{0:T(512)(128)(4,1)S(1)}, ...), condition=%wide.region_12.13_spmd.clone.clone, body=%wide.region_5.0_spmd.clone.clone.sunk | while | flops 48931344 | bytes 74002920 | solution.py:99
  244.2 54.5 %conditional.4 = (f32[512,4096]{0,1:T(8,128)}) conditional(s32[]{:T(128)} %bitcast.102, f32[512,4096]{0,1:T(8,128)} %get-tuple-element.358, (s32[]{:T(128)}, s32[4]{0:T(128)S(1)}, s32[]{:T(128)}, s32[32,2048]{1,0:T(8,128)}, s32[512]{0:T(512)S(1)}, /*index=5*/s32[512]{0:T(512)S(1)}, s32[256]{0:T(256)S(1)}, s32[8]{0:T(128)S(1)}, ...), branch_computations={%region_6.6_spmd, %region_7.11_spmd.clone} | conditional | flops 48931340 | bytes 73999632 | solution.py:92
  247.8 1.8 fusion.9
  249.7 1.9 copy.75
  251.6 3.6 gather_fusion
  255.2 4.5 broadcast_select_fusion
  259.7 5.4 %copy.76 = f32[512,2048]{0,1:T(8,128)} copy(f32[512,2048]{1,0:T(8,128)} %broadcast_select_fusion) | data formatting | bytes 8388608 | tf_op jit(solution)/shard_map/while/body/eval_jaxpr/cond/branch_1_fun/jit(_take)/select_n | solution.py:65
  266.8 20.2 %gather_fusion.1 = f32[4096,512]{1,0:T(8,128)} fusion(f32[512,2048]{0,1:T(8,128)} %copy.76, s32[4096]{0:T(1024)S(1)} %broadcast_clamp_fusion), kind=kCustom, calls=%fused_computation.1.clone | custom fusion | bytes 16793600 | tf_op jit(solution)/shard_map/while/body/eval_jaxpr/cond/branch_1_fun/jit(_take)/gather | solution.py:65
  288.0 10.8 %fusion.6 = f32[512,4096]{0,1:T(8,128)} fusion(f32[512,4096]{0,1:T(8,128)} %get-tuple-element.268, f32[4096,512]{1,0:T(8,128)} %gather_fusion.1, pred[4096]{0:T(1024)(128)(4,1)S(1)} %compare_and_fusion, pred[512]{0:T(512)(128)(4,1)S(1)} %compare_reduce_fusion.1, pred[4096]{0:T(1024)(128)(4,1)S(1)} %bitcast.113), kind=kLoop, calls=%fused_computation.7 | loop fusion | flops 8388608 | bytes 25174528 | tf_op jit(solution)/shard_map/while/body/eval_jaxpr/cond/branch_1_fun/add | solution.py:66
  300.0 54.5 %conditional.4 = (f32[512,4096]{0,1:T(8,128)}) conditional(s32[]{:T(128)} %bitcast.102, f32[512,4096]{0,1:T(8,128)} %get-tuple-element.358, (s32[]{:T(128)}, s32[4]{0:T(128)S(1)}, s32[]{:T(128)}, s32[32,2048]{1,0:T(8,128)}, s32[512]{0:T(512)S(1)}, /*index=5*/s32[512]{0:T(512)S(1)}, s32[256]{0:T(256)S(1)}, s32[8]{0:T(128)S(1)}, ...), branch_computations={%region_6.6_spmd, %region_7.11_spmd.clone} | conditional | flops 48931340 | bytes 73999632 | solution.py:92
  303.6 1.8 fusion.9
  305.5 1.9 copy.75
  307.4 3.6 gather_fusion
  311.0 4.5 broadcast_select_fusion
  315.5 5.4 %copy.76 = f32[512,2048]{0,1:T(8,128)} copy(f32[512,2048]{1,0:T(8,128)} %broadcast_select_fusion) | data formatting | bytes 8388608 | tf_op jit(solution)/shard_map/while/body/eval_jaxpr/cond/branch_1_fun/jit(_take)/select_n | solution.py:65
  322.6 20.2 %gather_fusion.1 = f32[4096,512]{1,0:T(8,128)} fusion(f32[512,2048]{0,1:T(8,128)} %copy.76, s32[4096]{0:T(1024)S(1)} %broadcast_clamp_fusion), kind=kCustom, calls=%fused_computation.1.clone | custom fusion | bytes 16793600 | tf_op jit(solution)/shard_map/while/body/eval_jaxpr/cond/branch_1_fun/jit(_take)/gather | solution.py:65
  343.8 10.8 %fusion.6 = f32[512,4096]{0,1:T(8,128)} fusion(f32[512,4096]{0,1:T(8,128)} %get-tuple-element.268, f32[4096,512]{1,0:T(8,128)} %gather_fusion.1, pred[4096]{0:T(1024)(128)(4,1)S(1)} %compare_and_fusion, pred[512]{0:T(512)(128)(4,1)S(1)} %compare_reduce_fusion.1, pred[4096]{0:T(1024)(128)(4,1)S(1)} %bitcast.113), kind=kLoop, calls=%fused_computation.7 | loop fusion | flops 8388608 | bytes 25174528 | tf_op jit(solution)/shard_map/while/body/eval_jaxpr/cond/branch_1_fun/add | solution.py:66
  355.8 54.5 %conditional.4 = (f32[512,4096]{0,1:T(8,128)}) conditional(s32[]{:T(128)} %bitcast.102, f32[512,4096]{0,1:T(8,128)} %get-tuple-element.358, (s32[]{:T(128)}, s32[4]{0:T(128)S(1)}, s32[]{:T(128)}, s32[32,2048]{1,0:T(8,128)}, s32[512]{0:T(512)S(1)}, /*index=5*/s32[512]{0:T(512)S(1)}, s32[256]{0:T(256)S(1)}, s32[8]{0:T(128)S(1)}, ...), branch_computations={%region_6.6_spmd, %region_7.11_spmd.clone} | conditional | flops 48931340 | bytes 73999632 | solution.py:92
  359.4 1.8 fusion.9
  361.3 1.9 copy.75
  363.2 3.6 gather_fusion
  366.8 4.5 broadcast_select_fusion
  371.3 5.4 %copy.76 = f32[512,2048]{0,1:T(8,128)} copy(f32[512,2048]{1,0:T(8,128)} %broadcast_select_fusion) | data formatting | bytes 8388608 | tf_op jit(solution)/shard_map/while/body/eval_jaxpr/cond/branch_1_fun/jit(_take)/select_n | solution.py:65
  378.4 20.2 %gather_fusion.1 = f32[4096,512]{1,0:T(8,128)} fusion(f32[512,2048]{0,1:T(8,128)} %copy.76, s32[4096]{0:T(1024)S(1)} %broadcast_clamp_fusion), kind=kCustom, calls=%fused_computation.1.clone | custom fusion | bytes 16793600 | tf_op jit(solution)/shard_map/while/body/eval_jaxpr/cond/branch_1_fun/jit(_take)/gather | solution.py:65
  399.6 10.8 %fusion.6 = f32[512,4096]{0,1:T(8,128)} fusion(f32[512,4096]{0,1:T(8,128)} %get-tuple-element.268, f32[4096,512]{1,0:T(8,128)} %gather_fusion.1, pred[4096]{0:T(1024)(128)(4,1)S(1)} %compare_and_fusion, pred[512]{0:T(512)(128)(4,1)S(1)} %compare_reduce_fusion.1, pred[4096]{0:T(1024)(128)(4,1)S(1)} %bitcast.113), kind=kLoop, calls=%fused_computation.7 | loop fusion | flops 8388608 | bytes 25174528 | tf_op jit(solution)/shard_map/while/body/eval_jaxpr/cond/branch_1_fun/add | solution.py:66
  411.6 54.5 %conditional.4 = (f32[512,4096]{0,1:T(8,128)}) conditional(s32[]{:T(128)} %bitcast.102, f32[512,4096]{0,1:T(8,128)} %get-tuple-element.358, (s32[]{:T(128)}, s32[4]{0:T(128)S(1)}, s32[]{:T(128)}, s32[32,2048]{1,0:T(8,128)}, s32[512]{0:T(512)S(1)}, /*index=5*/s32[512]{0:T(512)S(1)}, s32[256]{0:T(256)S(1)}, s32[8]{0:T(128)S(1)}, ...), branch_computations={%region_6.6_spmd, %region_7.11_spmd.clone} | conditional | flops 48931340 | bytes 73999632 | solution.py:92
  415.2 1.8 fusion.9
  417.1 1.9 copy.75
  419.0 3.6 gather_fusion
  422.6 4.5 broadcast_select_fusion
  427.1 5.4 %copy.76 = f32[512,2048]{0,1:T(8,128)} copy(f32[512,2048]{1,0:T(8,128)} %broadcast_select_fusion) | data formatting | bytes 8388608 | tf_op jit(solution)/shard_map/while/body/eval_jaxpr/cond/branch_1_fun/jit(_take)/select_n | solution.py:65
  434.2 20.2 %gather_fusion.1 = f32[4096,512]{1,0:T(8,128)} fusion(f32[512,2048]{0,1:T(8,128)} %copy.76, s32[4096]{0:T(1024)S(1)} %broadcast_clamp_fusion), kind=kCustom, calls=%fused_computation.1.clone | custom fusion | bytes 16793600 | tf_op jit(solution)/shard_map/while/body/eval_jaxpr/cond/branch_1_fun/jit(_take)/gather | solution.py:65
  455.4 10.8 %fusion.6 = f32[512,4096]{0,1:T(8,128)} fusion(f32[512,4096]{0,1:T(8,128)} %get-tuple-element.268, f32[4096,512]{1,0:T(8,128)} %gather_fusion.1, pred[4096]{0:T(1024)(128)(4,1)S(1)} %compare_and_fusion, pred[512]{0:T(512)(128)(4,1)S(1)} %compare_reduce_fusion.1, pred[4096]{0:T(1024)(128)(4,1)S(1)} %bitcast.113), kind=kLoop, calls=%fused_computation.7 | loop fusion | flops 8388608 | bytes 25174528 | tf_op jit(solution)/shard_map/while/body/eval_jaxpr/cond/branch_1_fun/add | solution.py:66
  466.2 8.9 %copy.72 = f32[512,4096]{1,0:T(8,128)} copy(f32[512,4096]{0,1:T(8,128)} %get-tuple-element.219) | data formatting | bytes 16777216 | tf_op jit(solution)/shard_map/while | solution.py:99
  475.1 8.1 %fusion.19 = bf16[1,512,4096]{2,1,0:T(8,128)(2,1)} fusion(f32[512,4096]{1,0:T(8,128)} %copy.72, bf16[1,512,4096]{2,1,0:T(8,128)(2,1)} %param.19), kind=kLoop, calls=%fused_computation.38 | loop fusion | flops 6291456 | bytes 16777216 | tf_op jit(solution)/shard_map/broadcast_in_dim | solution.py:101
  (142 shorter events, 30.7 us)
Async XLA Ops:
  6.5 57.1 %copy-start = (bf16[1,256,2048]{2,1,0:T(8,128)(2,1)S(1)}, bf16[1,256,2048]{2,1,0:T(8,128)(2,1)}, u32[]{:S(2)}) copy-start(bf16[1,256,2048]{2,1,0:T(8,128)(2,1)} %param.12) | copy-start | bytes 3145732
  6.5 57.1 %all-gather.3.cloned.1.call-start = ((), (), s32[]{:S(2)}) async-start(), calls=%async_computation.2 | async-start | bytes 9437184 | tf_op jit(solution)/shard_map/all_gather | solution.py:24
  7.3 63.2 %copy-start.3 = (s32[32]{0:T(128)S(1)}, s32[32]{0:T(128)}, u32[]{:S(2)}) copy-start(s32[32]{0:T(128)} %param.18) | copy-start | bytes 388
  7.3 115.7 %copy-start.4 = (f32[1,2048]{1,0:T(1,128)S(1)}, f32[1,2048]{1,0:T(1,128)}, u32[]{:S(2)}) copy-start(f32[1,2048]{1,0:T(1,128)} %param.14) | copy-start | bytes 24580
  7.3 115.7 %all-gather.5.cloned.1.call-start = ((), (), s32[]{:S(2)}) async-start(), calls=%async_computation.3 | async-start | bytes 9437184 | tf_op jit(solution)/shard_map/all_gather | solution.py:29
  123.0 6.7 %copy-start.2 = (f32[1,1,8,32,256]{4,3,2,1,0:T(8,128)S(1)}, f32[1,1,8,32,256]{4,3,2,1,0:T(8,128)}, u32[]{:S(2)}) copy-start(f32[1,1,8,32,256]{4,3,2,1,0:T(8,128)} %param.16) | copy-start | bytes 786436
  181.1 20.7 %all-to-all-start = ((bf16[32,2,2048]{2,1,0:T(2,128)(2,1)}), bf16[32,2,2048]{2,1,0:T(2,128)(2,1)S(1)}, u32[]{:S(2)}, u32[]{:S(2)}) async-start(bf16[32,2,2048]{2,1,0:T(2,128)(2,1)} %reshape.271), calls=%async_computation | async-start | bytes 524288 | tf_op jit(solution)/shard_map/all_to_all | solution.py:81
  205.8 31.8 %all-to-all-start.1 = ((bf16[32,4,4096]{2,1,0:T(4,128)(2,1)}), bf16[32,4,4096]{2,1,0:T(4,128)(2,1)S(1)}, u32[]{:S(2)}, u32[]{:S(2)}) async-start(bf16[32,4,4096]{2,1,0:T(4,128)(2,1)} %select_select_fusion), calls=%async_computation.1 | async-start | bytes 2097152 | tf_op jit(solution)/shard_map/all_to_all | solution.py:86
  475.1 8.1 %copy-start.1 = (bf16[1,256,2048]{2,1,0:T(8,128)(2,1)S(1)}, bf16[1,256,2048]{2,1,0:T(8,128)(2,1)}, u32[]{:S(2)}) copy-start(bf16[1,256,2048]{2,1,0:T(8,128)(2,1)} %param.12) | copy-start | bytes 3145732
Sparse Core Ops, SparseCore 0:
  9.2 54.4 all-gather.2
  70.5 52.4 all-gather.4
where the time goes:
time: 492 us; the launch traced here: 490 us
  local copies, waits for them, and re-layouts  155 us (32%)
  waiting for transfers between devices  144 us (29%)
  other arithmetic  125 us (25%)
  matrix products  24.7 us (5%)
  starting transfers between devices  16.5 us (3%)
  between operations  13.6 us (3%)
  loops' own time  10.9 us (2%)
    gather x8, local copies, waits for them, and re-layouts, place(): picked = jnp.take(jnp.take(dense, source_rows, axis=0), source_cols, axis=1)  95.3 us
    all_gather x1, waiting for transfers between devices, body(): lax.all_gather(pivot_inverse, 'panel', axis=1, tiled=True)[0]  56.4 us
    all_gather x1, waiting for transfers between devices, body(): gathered = lax.all_gather(factor, 'panel', axis=0, tiled=True)  52.2 us
    add x4, other arithmetic, place(): total + jnp.where(valid_rows[:, None] & valid_cols[None, :], picked, 0.0)  43 us
    all_to_all x1, waiting for transfers between devices, body(): lax.all_to_all(outgoing, 'front', split_axis=0, concat_axis=2, tiled=True)  24.9 us
    another operation x4, other arithmetic, compress_rows(): lower = jnp.linalg.cholesky(gram)  23.6 us
    select_n x4, local copies, waits for them, and re-layouts, place(): picked = jnp.take(jnp.take(dense, source_rows, axis=0), source_cols, axis=1)  21.4 us
    another operation x3, other arithmetic, compress_rows(): basis = jax.scipy.linalg.solve_triangular(lower, range_t, lower=True)  19.8 us
  transfers between devices with their start and end apart: 4, of which 4 were waited for; matrix products, arithmetic and copies ran while one was open for 0% of the time, Pallas kernels for 0%

commit v1 on v0

--- a/solution.py
+++ b/solution.py
@@ -4,6 +4,11 @@
 from jax.sharding import PartitionSpec as P
 
 MAXKIDS = 4
+
+
+def all_by_exchange(array, axis, d):
+    outgoing = jnp.stack([array] * lax.axis_size(axis))
+    return jnp.concatenate(lax.all_to_all(outgoing, axis, 0, 0), axis=d)
 
 
 def compress_rows(schur, omega, tile_rows, tile_cols, tile_size):
@@ -26,7 +31,7 @@
     )
     factor = factor_sum.astype(jnp.bfloat16)
     scaled = (factor.astype(jnp.float32) / pivots[0][None, :]).astype(jnp.bfloat16)
-    gathered = lax.all_gather(factor, "panel", axis=0, tiled=True)
+    gathered = all_by_exchange(factor, "panel", 0)
     update = lax.dot_general(
         scaled, gathered, (((1,), (1,)), ((), ())), preferred_element_type=jnp.float32
     )

time: 492 us -> 542 us (1.10)
  waiting for transfers between devices: 144 us -> 186 us
    all_to_all x0 -> x1, waiting for transfers between devices: none -> 94.2 us  [all_by_exchange(): return jnp.concatenate(lax.all_to_all(outgoing, axis, 0, 0), axis=d)]
    all_gather x1 -> x0, waiting for transfers between devices: 52.2 us -> none  [body(): gathered = lax.all_gather(factor, 'panel', axis=0, tiled=True)]
where the time goes in v1:
time: 542 us; the launch traced here: 540 us
  waiting for transfers between devices  186 us (34%)
  local copies, waits for them, and re-layouts  160 us (30%)
  other arithmetic  125 us (23%)
  matrix products  23.5 us (4%)
  starting transfers between devices  21.4 us (4%)
  between operations  13.6 us (3%)
  loops' own time  10.9 us (2%)
    gather x8, local copies, waits for them, and re-layouts, place(): picked = jnp.take(jnp.take(dense, source_rows, axis=0), source_cols, axis=1)  95.3 us
    all_to_all x1, waiting for transfers between devices, all_by_exchange(): return jnp.concatenate(lax.all_to_all(outgoing, axis, 0, 0), axis=d)  94.2 us
    all_gather x1, waiting for transfers between devices, body(): lax.all_gather(pivot_inverse, 'panel', axis=1, tiled=True)[0]  56.4 us
    add x4, other arithmetic, place(): total + jnp.where(valid_rows[:, None] & valid_cols[None, :], picked, 0.0)  43 us
    all_to_all x1, waiting for transfers between devices, body(): lax.all_to_all(outgoing, 'front', split_axis=0, concat_axis=2, tiled=True)  24.7 us
    another operation x4, other arithmetic, compress_rows(): lower = jnp.linalg.cholesky(gram)  23.6 us
    select_n x4, local copies, waits for them, and re-layouts, place(): picked = jnp.take(jnp.take(dense, source_rows, axis=0), source_cols, axis=1)  21.4 us
    another operation x3, other arithmetic, compress_rows(): basis = jax.scipy.linalg.solve_triangular(lower, range_t, lower=True)  19.8 us
  transfers between devices with their start and end apart: 4, of which 4 were waited for; matrix products, arithmetic and copies ran while one was open for 0% of the time, Pallas kernels for 0%

profile of v1, /device:TPU:66, one launch (start us, length us, event | category | flops | bytes accessed | tf_op | source)
XLA Modules:
  0.0 540.2 jit_solution(18016392612269333732)
XLA Ops:
  7.3 56.4 %all-gather.2.cloned.1.call-done = bf16[1,2048,2048]{2,1,0:T(8,128)(2,1)} async-done(((bf16[1,256,2048]{2,1,0:T(8,128)(2,1)}), bf16[1,2048,2048]{2,1,0:T(8,128)(2,1)}) %all-gather.2.cloned.1.call-update) | async-done | bytes 8388624 | tf_op jit(solution)/shard_map/all_gather | solution.py:29
  63.7 5.7 %fusion.20 = bf16[256,2048]{1,0:T(8,128)(2,1)S(1)} fusion(bf16[1,2048,2048]{2,1,0:T(8,128)(2,1)} %all-gather.2.cloned.1.call-done, bf16[1,256,2048]{2,1,0:T(8,128)(2,1)S(1)} %copy-done), kind=kOutput, calls=%fused_computation.40 | convolution fusion | flops 2148007936 | bytes 10485760 | tf_op jit(solution)/shard_map/dot_general | solution.py:27
  70.4 4.3 stack.8
  74.6 5.1 all-to-all-start
  80.1 94.2 %all-to-all-done = bf16[8,256,2048]{2,1,0:T(8,128)(2,1)} async-done(((bf16[8,256,2048]{2,1,0:T(8,128)(2,1)}), bf16[8,256,2048]{2,1,0:T(8,128)(2,1)}, u32[]{:S(2)}, u32[]{:S(2)}) %all-to-all-start) | async-done | bytes 8388640 | tf_op jit(solution)/shard_map/all_to_all | solution.py:11
  174.3 6.4 %convolution_subtract_fusion = f32[256,2048]{1,0:T(8,128)S(1)} fusion(bf16[2048,2048]{1,0:T(8,128)(2,1)} %bitcast.16, f32[1,256,2048]{2,1,0:T(8,128)} %param.15, bf16[256,2048]{1,0:T(8,128)(2,1)S(1)} %copy-done.3, f32[2048]{0:T(1024)S(1)} %bitcast.119), kind=kOutput, calls=%fused_computation.39 | convolution fusion | flops 2149580800 | bytes 13639680 | tf_op jit(solution)/shard_map/dot_general | solution.py:35
  180.7 2.0 fusion.25
  183.3 23.4 %custom-call.8 = f32[1,8,32,32]{3,2,1,0:T(8,128)S(1)} custom-call(f32[1,8,32,32]{3,2,1,0:T(8,128)S(1)} %fusion.38), custom_call_target="Cholesky" | custom-call | tf_op jit(solution)/shard_map/jit(cholesky)/cholesky | solution.py:18
  207.0 19.7 %custom-call.9 = f32[8,1,32,32]{2,3,1,0:T(8,128)S(1)} custom-call(f32[8,1,32,32]{3,2,1,0:T(8,128)S(1)} %select_bitcast_fusion), custom_call_target="InvertDiagBlocksLowerTriangular" | custom-call | tf_op jit(solution)/shard_map/jit(_solve_triangular)/vmap()/triangular_solve | solution.py:19
  229.1 2.2 reduce.17
  232.2 10.0 %all-to-all-start.1 = ((bf16[32,2,2048]{2,1,0:T(2,128)(2,1)}), bf16[32,2,2048]{2,1,0:T(2,128)(2,1)S(1)}, u32[]{:S(2)}, u32[]{:S(2)}) async-start(bf16[32,2,2048]{2,1,0:T(2,128)(2,1)} %reshape.277), calls=%async_computation.1 | async-start | bytes 524288 | tf_op jit(solution)/shard_map/all_to_all | solution.py:86
  242.8 9.5 %all-to-all-done.1 = bf16[32,2,2048]{2,1,0:T(2,128)(2,1)S(1)} async-done(((bf16[32,2,2048]{2,1,0:T(2,128)(2,1)}), bf16[32,2,2048]{2,1,0:T(2,128)(2,1)S(1)}, u32[]{:S(2)}, u32[]{:S(2)}) %all-to-all-start.1) | async-done | bytes 262176 | tf_op jit(solution)/shard_map/all_to_all | solution.py:86
  256.2 6.4 %all-to-all-start.2 = ((bf16[32,4,4096]{2,1,0:T(4,128)(2,1)}), bf16[32,4,4096]{2,1,0:T(4,128)(2,1)S(1)}, u32[]{:S(2)}, u32[]{:S(2)}) async-start(bf16[32,4,4096]{2,1,0:T(4,128)(2,1)} %select_select_fusion), calls=%async_computation.2 | async-start | bytes 2097152 | tf_op jit(solution)/shard_map/all_to_all | solution.py:91
  263.0 24.7 %all-to-all-done.2 = bf16[32,4,4096]{2,1,0:T(4,128)(2,1)S(1)} async-done(((bf16[32,4,4096]{2,1,0:T(4,128)(2,1)}), bf16[32,4,4096]{2,1,0:T(4,128)(2,1)S(1)}, u32[]{:S(2)}, u32[]{:S(2)}) %all-to-all-start.2) | async-done | bytes 1048608 | tf_op jit(solution)/shard_map/all_to_all | solution.py:91
  288.8 4.3 broadcast_in_dim.118
  293.1 223.2 %while.18 = (s32[]{:T(128)}, f32[512,4096]{0,1:T(8,128)}, pred[4]{0:T(512)(128)(4,1)S(1)}, s32[4]{0:T(128)S(1)}, s32[]{:T(128)}, /*index=5*/s32[32,2048]{1,0:T(8...) while((s32[]{:T(128)}, f32[512,4096]{0,1:T(8,128)}, pred[4]{0:T(512)(128)(4,1)S(1)}, ...), condition=%wide.region_12.13_spmd.clone.clone, body=%wide.region_5.0_spmd.clone.clone.sunk | while | flops 48931344 | bytes 74002920 | solution.py:104
  294.3 54.5 %conditional.4 = (f32[512,4096]{0,1:T(8,128)}) conditional(s32[]{:T(128)} %bitcast.103, f32[512,4096]{0,1:T(8,128)} %get-tuple-element.358, (s32[]{:T(128)}, s32[4]{0:T(128)S(1)}, s32[]{:T(128)}, s32[32,2048]{1,0:T(8,128)}, s32[512]{0:T(512)S(1)}, /*index=5*/s32[512]{0:T(512)S(1)}, s32[256]{0:T(256)S(1)}, s32[8]{0:T(128)S(1)}, ...), branch_computations={%region_6.6_spmd, %region_7.11_spmd.clone} | conditional | flops 48931340 | bytes 73999632 | solution.py:97
  298.0 1.8 fusion.9
  299.8 1.9 copy.75
  301.7 3.6 gather_fusion
  305.3 4.5 broadcast_select_fusion
  309.8 5.4 copy.76
  316.9 20.2 %gather_fusion.1 = f32[4096,512]{1,0:T(8,128)} fusion(f32[512,2048]{0,1:T(8,128)} %copy.76, s32[4096]{0:T(1024)S(1)} %broadcast_clamp_fusion), kind=kCustom, calls=%fused_computation.1.clone | custom fusion | bytes 16793600 | tf_op jit(solution)/shard_map/while/body/eval_jaxpr/cond/branch_1_fun/jit(_take)/gather | solution.py:70
  338.1 10.8 %fusion.6 = f32[512,4096]{0,1:T(8,128)} fusion(f32[512,4096]{0,1:T(8,128)} %get-tuple-element.268, f32[4096,512]{1,0:T(8,128)} %gather_fusion.1, pred[4096]{0:T(1024)(128)(4,1)S(1)} %compare_and_fusion, pred[512]{0:T(512)(128)(4,1)S(1)} %compare_reduce_fusion.1, pred[4096]{0:T(1024)(128)(4,1)S(1)} %bitcast.114), kind=kLoop, calls=%fused_computation.7 | loop fusion | flops 8388608 | bytes 25174528 | tf_op jit(solution)/shard_map/while/body/eval_jaxpr/cond/branch_1_fun/add | solution.py:71
  350.1 54.5 %conditional.4 = (f32[512,4096]{0,1:T(8,128)}) conditional(s32[]{:T(128)} %bitcast.103, f32[512,4096]{0,1:T(8,128)} %get-tuple-element.358, (s32[]{:T(128)}, s32[4]{0:T(128)S(1)}, s32[]{:T(128)}, s32[32,2048]{1,0:T(8,128)}, s32[512]{0:T(512)S(1)}, /*index=5*/s32[512]{0:T(512)S(1)}, s32[256]{0:T(256)S(1)}, s32[8]{0:T(128)S(1)}, ...), branch_computations={%region_6.6_spmd, %region_7.11_spmd.clone} | conditional | flops 48931340 | bytes 73999632 | solution.py:97
  353.8 1.8 fusion.9
  355.6 1.9 copy.75
  357.5 3.6 gather_fusion
  361.1 4.5 broadcast_select_fusion
  365.6 5.4 copy.76
  372.7 20.2 %gather_fusion.1 = f32[4096,512]{1,0:T(8,128)} fusion(f32[512,2048]{0,1:T(8,128)} %copy.76, s32[4096]{0:T(1024)S(1)} %broadcast_clamp_fusion), kind=kCustom, calls=%fused_computation.1.clone | custom fusion | bytes 16793600 | tf_op jit(solution)/shard_map/while/body/eval_jaxpr/cond/branch_1_fun/jit(_take)/gather | solution.py:70
  393.9 10.8 %fusion.6 = f32[512,4096]{0,1:T(8,128)} fusion(f32[512,4096]{0,1:T(8,128)} %get-tuple-element.268, f32[4096,512]{1,0:T(8,128)} %gather_fusion.1, pred[4096]{0:T(1024)(128)(4,1)S(1)} %compare_and_fusion, pred[512]{0:T(512)(128)(4,1)S(1)} %compare_reduce_fusion.1, pred[4096]{0:T(1024)(128)(4,1)S(1)} %bitcast.114), kind=kLoop, calls=%fused_computation.7 | loop fusion | flops 8388608 | bytes 25174528 | tf_op jit(solution)/shard_map/while/body/eval_jaxpr/cond/branch_1_fun/add | solution.py:71
  405.9 54.5 %conditional.4 = (f32[512,4096]{0,1:T(8,128)}) conditional(s32[]{:T(128)} %bitcast.103, f32[512,4096]{0,1:T(8,128)} %get-tuple-element.358, (s32[]{:T(128)}, s32[4]{0:T(128)S(1)}, s32[]{:T(128)}, s32[32,2048]{1,0:T(8,128)}, s32[512]{0:T(512)S(1)}, /*index=5*/s32[512]{0:T(512)S(1)}, s32[256]{0:T(256)S(1)}, s32[8]{0:T(128)S(1)}, ...), branch_computations={%region_6.6_spmd, %region_7.11_spmd.clone} | conditional | flops 48931340 | bytes 73999632 | solution.py:97
  411.4 1.9 copy.75
  413.3 3.6 gather_fusion
  416.9 4.5 broadcast_select_fusion
  421.4 5.4 copy.76
  428.5 20.2 %gather_fusion.1 = f32[4096,512]{1,0:T(8,128)} fusion(f32[512,2048]{0,1:T(8,128)} %copy.76, s32[4096]{0:T(1024)S(1)} %broadcast_clamp_fusion), kind=kCustom, calls=%fused_computation.1.clone | custom fusion | bytes 16793600 | tf_op jit(solution)/shard_map/while/body/eval_jaxpr/cond/branch_1_fun/jit(_take)/gather | solution.py:70
  449.7 10.8 %fusion.6 = f32[512,4096]{0,1:T(8,128)} fusion(f32[512,4096]{0,1:T(8,128)} %get-tuple-element.268, f32[4096,512]{1,0:T(8,128)} %gather_fusion.1, pred[4096]{0:T(1024)(128)(4,1)S(1)} %compare_and_fusion, pred[512]{0:T(512)(128)(4,1)S(1)} %compare_reduce_fusion.1, pred[4096]{0:T(1024)(128)(4,1)S(1)} %bitcast.114), kind=kLoop, calls=%fused_computation.7 | loop fusion | flops 8388608 | bytes 25174528 | tf_op jit(solution)/shard_map/while/body/eval_jaxpr/cond/branch_1_fun/add | solution.py:71
  461.7 54.5 %conditional.4 = (f32[512,4096]{0,1:T(8,128)}) conditional(s32[]{:T(128)} %bitcast.103, f32[512,4096]{0,1:T(8,128)} %get-tuple-element.358, (s32[]{:T(128)}, s32[4]{0:T(128)S(1)}, s32[]{:T(128)}, s32[32,2048]{1,0:T(8,128)}, s32[512]{0:T(512)S(1)}, /*index=5*/s32[512]{0:T(512)S(1)}, s32[256]{0:T(256)S(1)}, s32[8]{0:T(128)S(1)}, ...), branch_computations={%region_6.6_spmd, %region_7.11_spmd.clone} | conditional | flops 48931340 | bytes 73999632 | solution.py:97
  467.2 1.9 copy.75
  469.1 3.6 gather_fusion
  472.7 4.5 broadcast_select_fusion
  477.2 5.4 copy.76
  484.3 20.2 %gather_fusion.1 = f32[4096,512]{1,0:T(8,128)} fusion(f32[512,2048]{0,1:T(8,128)} %copy.76, s32[4096]{0:T(1024)S(1)} %broadcast_clamp_fusion), kind=kCustom, calls=%fused_computation.1.clone | custom fusion | bytes 16793600 | tf_op jit(solution)/shard_map/while/body/eval_jaxpr/cond/branch_1_fun/jit(_take)/gather | solution.py:70
  505.5 10.8 %fusion.6 = f32[512,4096]{0,1:T(8,128)} fusion(f32[512,4096]{0,1:T(8,128)} %get-tuple-element.268, f32[4096,512]{1,0:T(8,128)} %gather_fusion.1, pred[4096]{0:T(1024)(128)(4,1)S(1)} %compare_and_fusion, pred[512]{0:T(512)(128)(4,1)S(1)} %compare_reduce_fusion.1, pred[4096]{0:T(1024)(128)(4,1)S(1)} %bitcast.114), kind=kLoop, calls=%fused_computation.7 | loop fusion | flops 8388608 | bytes 25174528 | tf_op jit(solution)/shard_map/while/body/eval_jaxpr/cond/branch_1_fun/add | solution.py:71
  516.3 8.9 %copy.72 = f32[512,4096]{1,0:T(8,128)} copy(f32[512,4096]{0,1:T(8,128)} %get-tuple-element.219) | data formatting | bytes 16777216 | tf_op jit(solution)/shard_map/while | solution.py:104
  525.2 8.1 %fusion.19 = bf16[1,512,4096]{2,1,0:T(8,128)(2,1)} fusion(f32[512,4096]{1,0:T(8,128)} %copy.72, bf16[1,512,4096]{2,1,0:T(8,128)(2,1)} %param.19), kind=kLoop, calls=%fused_computation.38 | loop fusion | flops 6291456 | bytes 16777216 | tf_op jit(solution)/shard_map/broadcast_in_dim | solution.py:106
  (146 shorter events, 35.2 us)
Async XLA Ops:
  6.5 57.1 %copy-start = (bf16[1,256,2048]{2,1,0:T(8,128)(2,1)S(1)}, bf16[1,256,2048]{2,1,0:T(8,128)(2,1)}, u32[]{:S(2)}) copy-start(bf16[1,256,2048]{2,1,0:T(8,128)(2,1)} %param.12) | copy-start | bytes 3145732
  6.5 57.1 %all-gather.2.cloned.1.call-start = ((), (), s32[]{:S(2)}) async-start(), calls=%async_computation.3 | async-start | bytes 9437184 | tf_op jit(solution)/shard_map/all_gather | solution.py:29
  69.4 1.0 copy-start.2
  74.6 5.1 copy-start.5
  74.6 99.7 %copy-start.3 = (bf16[256,2048]{1,0:T(8,128)(2,1)S(1)}, bf16[256,2048]{1,0:T(8,128)(2,1)}, u32[]{:S(2)}) copy-start(bf16[256,2048]{1,0:T(8,128)(2,1)} %copy-done.2) | copy-start | bytes 3145732
  74.6 99.7 %copy-start.6 = (f32[1,2048]{1,0:T(1,128)S(1)}, f32[1,2048]{1,0:T(1,128)}, u32[]{:S(2)}) copy-start(f32[1,2048]{1,0:T(1,128)} %param.14) | copy-start | bytes 24580
  74.6 99.7 %all-to-all-start = ((bf16[8,256,2048]{2,1,0:T(8,128)(2,1)}), bf16[8,256,2048]{2,1,0:T(8,128)(2,1)}, u32[]{:S(2)}, u32[]{:S(2)}) async-start(bf16[8,256,2048]{2,1,0:T(8,128)(2,1)} %stack.8), calls=%async_computation | async-start | bytes 16777216 | tf_op jit(solution)/shard_map/all_to_all | solution.py:11
  174.3 6.4 %copy-start.4 = (f32[1,1,8,32,256]{4,3,2,1,0:T(8,128)S(1)}, f32[1,1,8,32,256]{4,3,2,1,0:T(8,128)}, u32[]{:S(2)}) copy-start(f32[1,1,8,32,256]{4,3,2,1,0:T(8,128)} %param.16) | copy-start | bytes 786436
  232.2 20.1 %all-to-all-start.1 = ((bf16[32,2,2048]{2,1,0:T(2,128)(2,1)}), bf16[32,2,2048]{2,1,0:T(2,128)(2,1)S(1)}, u32[]{:S(2)}, u32[]{:S(2)}) async-start(bf16[32,2,2048]{2,1,0:T(2,128)(2,1)} %reshape.277), calls=%async_computation.1 | async-start | bytes 524288 | tf_op jit(solution)/shard_map/all_to_all | solution.py:86
  256.2 31.5 %all-to-all-start.2 = ((bf16[32,4,4096]{2,1,0:T(4,128)(2,1)}), bf16[32,4,4096]{2,1,0:T(4,128)(2,1)S(1)}, u32[]{:S(2)}, u32[]{:S(2)}) async-start(bf16[32,4,4096]{2,1,0:T(4,128)(2,1)} %select_select_fusion), calls=%async_computation.2 | async-start | bytes 2097152 | tf_op jit(solution)/shard_map/all_to_all | solution.py:91
  525.2 8.1 %copy-start.1 = (bf16[1,256,2048]{2,1,0:T(8,128)(2,1)S(1)}, bf16[1,256,2048]{2,1,0:T(8,128)(2,1)}, u32[]{:S(2)}) copy-start(bf16[1,256,2048]{2,1,0:T(8,128)(2,1)} %param.12) | copy-start | bytes 3145732
Sparse Core Ops, SparseCore 0:
  9.2 54.4 all-gather.1
